TPU v7x, 32 devices: a whole 2x2x4 slice. The times are simulated.
32 devices in a mesh: px: 4 (over y, x), py: 8 (over z, core).
Axes of the slice: x: 2, y: 2, z: 4, core: 2. Of those that a mesh axis runs over, the one named last changes fastest.
Arguments:
- photons: float32 [1024, 128], P(('px', 'py')), may hold values from 50 to 1000
- halo_cells: int32 [1024, 128], P(('px', 'py')), may hold values from 0 to 1769471
- halo_counts: int32 [1024], P(('px', 'py')), may hold values from 1 to 128
- owners: int32 [1024, 1], P(('px', 'py')), may hold values from 0 to 7; in each aligned block of 32 rows (0 to 31, 32 to 63, ...) at most 4 rows name the same one
- density: float32 [384, 384, 384], P('px', 'py'), may hold values from 0.02 to 50
Outputs:
- fraction: float32 [384, 384, 384], P('px', 'py')
Inputs may be any that keep to these rules, and one draw needn't show every extreme that they name: The halos of a block all lie in pencil owners[b] of the block's own slab. Among the 32 blocks of one device no owner appears more than 4 times, a bound that some block reaches. Slots at or past halo_counts[b] are not live and carry arbitrary values. `halo_cells`: A cell index within the owner pencil is (x * 48 + y) * 384 + z with x, y, z local to that pencil.
All inputs are finite; a program needn't handle non-finite values.
Results may differ from a plain program's by a relative error of at most 0.0003.
Values sent between devices are 32-bit elements; how exact they have to be, the bound alone decides.
A program may use at most 192 MiB of HBM per device.

v0:
```python
import jax
import jax.numpy as jnp
from jax import lax
from jax.sharding import PartitionSpec as P

NG = 384
SLOTS = 128
RADIUS = 20


def product(form, left, right):
    return jnp.einsum(form, left, right, precision=lax.Precision.HIGHEST)


def rotate(form, real_part, imag_part, cos_table, sin_table, direction):
    signed_sin = direction * sin_table
    first = product(form, real_part + imag_part, cos_table)
    second = product(form, real_part, signed_sin - cos_table)
    third = product(form, imag_part, cos_table + signed_sin)
    return (first - third, first + second)


def tables(length):
    index_row = jnp.arange(length, dtype=jnp.int32)
    angle = (index_row[:, None] * index_row[None, :] % length).astype(jnp.float32) * (
        2.0 * jnp.pi / length
    )
    return (jnp.cos(angle), jnp.sin(angle))


def signed_frequency(index_values):
    return jnp.where(index_values < NG // 2, index_values, index_values - NG).astype(jnp.float32)


def top_hat(freq_x, freq_y, freq_z):
    radial = jnp.sqrt(freq_x * freq_x + freq_y * freq_y + freq_z * freq_z) * (
        2.0 * jnp.pi * RADIUS / NG
    )
    safe = jnp.where(radial > 0, radial, 1.0)
    value = 3.0 * (jnp.sin(safe) - safe * jnp.cos(safe)) / (safe * safe * safe)
    return jnp.where(radial > 0, value, 1.0)


def paint(photon_rows, cell_rows, live_rows, cell_total):
    weights = jnp.where(live_rows, photon_rows, 0.0)
    empty = jnp.zeros((cell_total,), jnp.float32)
    return empty.at[cell_rows.reshape(-1)].add(weights.reshape(-1))


def on_device(photons, halo_cells, halo_counts, owners, density):
    rows_x, rows_y = (density.shape[0], density.shape[1])
    cell_total = rows_x * rows_y * NG
    count_x = lax.axis_size("px")
    count_y = lax.axis_size("py")
    place_y = lax.axis_index("py")
    slot_index = jnp.arange(SLOTS, dtype=jnp.int32)[None, :]
    all_photons, all_cells, all_counts, all_owners = (
        lax.all_gather(photons, "py", axis=0, tiled=True),
        lax.all_gather(halo_cells, "py", axis=0, tiled=True),
        lax.all_gather(halo_counts, "py", axis=0, tiled=True),
        lax.all_gather(owners, "py", axis=0, tiled=True),
    )
    live_rows = (slot_index < all_counts[:, None]) & (all_owners == place_y)
    painted = paint(all_photons, all_cells, live_rows, cell_total)
    cos_full, sin_full = tables(NG)
    field_rows = painted.reshape(rows_x * rows_y, NG)
    density_rows = density.reshape(rows_x * rows_y, NG)
    spec_real, spec_imag = rotate("az,zk->ka", field_rows, density_rows, cos_full, sin_full, -1.0)
    cos_y = cos_full.reshape(count_y, rows_y, NG)
    sin_y = sin_full.reshape(count_y, rows_y, NG)
    cos_x = cos_full.reshape(count_x, rows_x, NG)
    sin_x = sin_full.reshape(count_x, rows_x, NG)
    freq_all = signed_frequency(jnp.arange(NG, dtype=jnp.int32))
    devices_all = count_x * count_y
    slab_planes = NG // devices_all
    sent = (
        spec_real.reshape(devices_all, slab_planes, rows_x * rows_y),
        spec_imag.reshape(devices_all, slab_planes, rows_x * rows_y),
    )
    got_real, got_imag = (
        lax.all_to_all(sent[0], ("px", "py"), split_axis=0, concat_axis=2, tiled=True),
        lax.all_to_all(sent[1], ("px", "py"), split_axis=0, concat_axis=2, tiled=True),
    )
    got_real = got_real.reshape(slab_planes, count_x, count_y, rows_x, rows_y)
    got_imag = got_imag.reshape(slab_planes, count_x, count_y, rows_x, rows_y)
    plane_real, plane_imag = rotate("kiqxl,qlm->kixm", got_real, got_imag, cos_y, sin_y, -1.0)
    full_real, full_imag = rotate("kixm,ixn->kmn", plane_real, plane_imag, cos_x, sin_x, -1.0)
    freq_z = signed_frequency(
        lax.axis_index(("px", "py")) * slab_planes + jnp.arange(slab_planes, dtype=jnp.int32)
    )
    window = top_hat(freq_z[:, None, None], freq_all[None, :, None], freq_all[None, None, :])
    full_real = full_real * window
    full_imag = full_imag * window
    plane_real, plane_imag = rotate("kmn,ixn->kmix", full_real, full_imag, cos_x, sin_x, 1.0)
    back_real, back_imag = rotate("kmix,qlm->iqkxl", plane_real, plane_imag, cos_y, sin_y, 1.0)
    sent = (
        back_real.reshape(devices_all, slab_planes, rows_x * rows_y),
        back_imag.reshape(devices_all, slab_planes, rows_x * rows_y),
    )
    got_real, got_imag = (
        lax.all_to_all(sent[0], ("px", "py"), split_axis=0, concat_axis=1, tiled=True),
        lax.all_to_all(sent[1], ("px", "py"), split_axis=0, concat_axis=1, tiled=True),
    )
    got_real = got_real.reshape(NG, rows_x * rows_y)
    got_imag = got_imag.reshape(NG, rows_x * rows_y)
    final_real, final_imag = rotate("ka,kz->az", got_real, got_imag, cos_full, sin_full, 1.0)
    scale = 1.0 / (float(NG) * float(NG) * float(NG))
    photon_smooth = final_real * scale
    density_smooth = final_imag * scale
    fraction = jnp.clip(photon_smooth / jnp.maximum(density_smooth, 0.5), 0.0, 1.0)
    return fraction.reshape(rows_x, rows_y, NG)


def solution(mesh):
    placed = (
        P(("px", "py"), None),
        P(("px", "py"), None),
        P(("px", "py")),
        P(("px", "py"), None),
        P("px", "py", None),
    )
    return jax.shard_map(
        on_device, mesh=mesh, in_specs=placed, out_specs=P("px", "py", None), check_vma=False
    )
```

profile of v0, /device:TPU:0, one launch (start us, length us, event | category | flops | bytes accessed | tf_op | source)
XLA Modules:
  0.0 1580.6 jit_solution(1984231770731450605)
XLA Ops:
  0.0 15.9 %all_gather.15 = f32[256,128]{1,0:T(8,128)S(1)} all-gather(f32[32,128]{1,0:T(8,128)} %param.5), channel_id=1, replica_groups=mesh['px'=4,'py'=8] {'py'}, dimensions={0}, use_global_device_ids=true | all-gather | bytes 147456 | tf_op jit(solution)/shard_map/all_gather | solution.py:58
  15.9 14.2 all_gather.12
  42.8 174.8 %scatter_custom_fusion = f32[1769472]{0:T(1024)} fusion(s32[32768]{0:T(1024)S(1)} %bitcast.192, f32[32768]{0:T(1024)S(1)} %select_bitcast_fusion, f32[]{:T(128)} %constant.19.clone.1), kind=kCustom, calls=%fused_computation.47 | custom fusion | flops 32768 | bytes 7077892 | tf_op jit(solution)/shard_map/scatter-add | solution.py:47
  226.4 24.8 %fusion.29 = f32[384,4608]{1,0:T(8,128)S(1)} fusion(f32[4608,384]{1,0:T(8,128)} %reshape.184, f32[4608,384]{1,0:T(8,128)} %bitcast.189), kind=kOutput, calls=%fused_computation.45 | convolution fusion | flops 8156823552 | bytes 21233664 | tf_op jit(solution)/shard_map/az,zk->ka/dot_general | solution.py:12
  254.1 26.1 %convolution_add_fusion.1 = f32[384,4608]{1,0:T(8,128)} fusion(f32[384,4608]{1,0:T(8,128)S(1)} %fusion.29, f32[4608,384]{1,0:T(8,128)S(1)} %copy-done.6), kind=kOutput, calls=%fused_computation.11 | convolution fusion | flops 8157118464 | bytes 21233664 | tf_op jit(solution)/shard_map/az,zk->ka/dot_general | solution.py:12
  292.1 29.4 %convolution_subtract_fusion.1 = f32[384,4608]{1,0:T(8,128)} fusion(f32[384,4608]{1,0:T(8,128)} %copy-done.3, f32[4608,384]{1,0:T(8,128)} %bitcast.190), kind=kOutput, calls=%fused_computation.12 | convolution fusion | flops 8157118464 | bytes 21233664 | tf_op jit(solution)/shard_map/az,zk->ka/dot_general | solution.py:12
  329.5 169.9 %all-to-all-done.1 = f32[32,12,4608]{2,1,0:T(8,128)} async-done(((f32[32,12,4608]{2,1,0:T(8,128)}), f32[32,12,4608]{2,1,0:T(8,128)}, u32[]{:S(2)}, u32[]{:S(2)}) %all-to-all-start.1) | async-done | bytes 7077920 | tf_op jit(solution)/shard_map/all_to_all | solution.py:82
  508.5 10.7 copy.16
  519.2 26.0 %reshape.189 = f32[12,4,8,96,48]{4,3,2,1,0:T(8,128)} reshape(f32[1,12,32,4608]{3,2,1,0:T(8,128)} %copy.16) | data formatting | bytes 14155776 | tf_op jit(solution)/shard_map/reshape | solution.py:85
  545.3 165.4 %all-to-all-done = f32[32,12,4608]{2,1,0:T(8,128)} async-done(((f32[32,12,4608]{2,1,0:T(8,128)}), f32[32,12,4608]{2,1,0:T(8,128)}, u32[]{:S(2)}, u32[]{:S(2)}) %all-to-all-start) | async-done | bytes 7077920 | tf_op jit(solution)/shard_map/all_to_all | solution.py:81
  721.4 15.1 reshape.187
  736.5 26.2 %fusion.53 = f32[12,4,96,384,1]{3,2,4,1,0:T(8,128)} fusion(f32[12,4,8,96,48]{4,3,2,1,0:T(8,128)} %reshape.189, s32[8,48]{1,0:T(8,128)S(1)} %multiply_add_fusion), kind=kOutput, calls=%fused_computation.69 | convolution fusion | flops 8155348992 | bytes 14157312 | tf_op jit(solution)/shard_map/kiqxl,qlm->kixm/dot_general | solution.py:12
  762.7 27.8 %fusion = f32[12,4,96,384,1]{3,2,4,1,0:T(8,128)} fusion(f32[12,4,8,96,48]{4,3,2,1,0:T(8,128)S(1)} %copy-done, f32[12,4,8,96,48]{4,3,2,1,0:T(8,128)} %reshape.189, s32[8,48]{1,0:T(8,128)S(1)} %multiply_add_fusion), kind=kOutput, calls=%fused_computation.1 | convolution fusion | flops 8156823552 | bytes 21235200 | tf_op jit(solution)/shard_map/kiqxl,qlm->kixm/dot_general | solution.py:12
  790.5 22.9 %fusion.51 = f32[12,4,96,384,1]{3,2,4,1,0:T(8,128)} fusion(f32[12,4,8,96,48]{4,3,2,1,0:T(8,128)S(1)} %copy-done, s32[8,48]{1,0:T(8,128)S(1)} %multiply_add_fusion), kind=kOutput, calls=%fused_computation.67 | convolution fusion | flops 8155348992 | bytes 14157312 | tf_op jit(solution)/shard_map/kiqxl,qlm->kixm/dot_general | solution.py:12
  813.4 25.1 %fusion.27 = f32[12,384,384,1]{2,1,3,0:T(8,128)S(1)} fusion(f32[12,4,96,384,1]{3,2,4,1,0:T(8,128)} %fusion.53, f32[12,4,96,384,1]{3,2,4,1,0:T(8,128)} %fusion, f32[12,4,96,384,1]{3,2,4,1,0:T(8,128)} %fusion.51, s32[4,96]{1,0:T(4,128)S(1)} %multiply_add_fusion.1), kind=kOutput, calls=%fused_computation.43 | convolution fusion | flops 8160362496 | bytes 28313088 | tf_op jit(solution)/shard_map/kixm,ixn->kmn/dot_general | solution.py:12
  838.5 50.9 %fusion.21 = f32[12,384,384]{2,1,0:T(8,128)S(1)} fusion(f32[12,384,384,1]{2,1,3,0:T(8,128)S(1)} %fusion.27, f32[384]{0:T(512)S(1)} %fusion.197, f32[12,384]{1,0:T(8,128)S(1)} %broadcast_add_fusion, f32[12,4,96,384,1]{3,2,4,1,0:T(8,128)} %fusion.53, f32[12,4,96,384,1]{3,2,4,1,0:T(8,128)S(1)} %copy-done.7, f32[4,96,384,1]{2,1,0,3:T(8,128)S(1)} %fusion.272), kind=kOutput, calls=%fused_computation.33 | convolution fusion | flops 8178499584 | bytes 28921344 | tf_op jit(solution)/shard_map/kixm,ixn->kmn/dot_general | solution.py:12
  889.5 20.6 %fusion.11 = f32[12,384,4,96]{1,3,2,0:T(8,128)} fusion(f32[12,384,384]{2,1,0:T(8,128)S(1)} %fusion.21, s32[4,96]{1,0:T(4,128)S(1)} %multiply_add_fusion.1), kind=kOutput, calls=%fused_computation.22 | convolution fusion | flops 8155201536 | bytes 14157312 | tf_op jit(solution)/shard_map/kmn,ixn->kmix/dot_general | solution.py:12
  910.1 50.8 %fusion.22 = f32[12,384,384]{2,1,0:T(8,128)S(1)} fusion(f32[12,384,384,1]{2,1,3,0:T(8,128)} %copy-done.9, f32[384]{0:T(512)S(1)} %fusion.197, f32[12,384]{1,0:T(8,128)S(1)} %broadcast_add_fusion, f32[12,4,96,384,1]{3,2,4,1,0:T(8,128)S(1)} %bitcast.186, f32[12,4,96,384,1]{3,2,4,1,0:T(8,128)S(1)} %copy-done.7, f32[4,96,384,1]{2,1,0,3:T(8,128)S(1)} %fusion.274), kind=kOutput, calls=%fused_computation.35 | convolution fusion | flops 8178499584 | bytes 28921344 | tf_op jit(solution)/shard_map/kixm,ixn->kmn/dot_general | solution.py:12
  963.8 14.4 fusion.13
  978.3 20.0 %fusion.9 = f32[12,384,4,96]{1,3,2,0:T(8,128)S(1)} fusion(f32[12,384,384]{2,1,0:T(8,128)} %copy-done.8, s32[4,96]{1,0:T(4,128)S(1)} %multiply_add_fusion.1), kind=kOutput, calls=%fused_computation.20 | convolution fusion | flops 8155201536 | bytes 14157312 | tf_op jit(solution)/shard_map/kmn,ixn->kmix/dot_general | solution.py:12
  998.3 24.4 %fusion.19 = f32[8,48,12,4,96]{4,1,3,2,0:T(8,128)S(1)} fusion(f32[12,384,4,96]{1,3,2,0:T(8,128)S(1)} %fusion.13, f32[12,384,4,96]{1,3,2,0:T(8,128)S(1)} %fusion.9, f32[12,384,4,96]{1,3,2,0:T(8,128)} %fusion.11, s32[8,48]{1,0:T(8,128)S(1)} %multiply_add_fusion), kind=kOutput, calls=%fused_computation.30 | convolution fusion | flops 8160362496 | bytes 28313088 | tf_op jit(solution)/shard_map/kmix,qlm->iqkxl/dot_general | solution.py:12
  1026.4 24.8 %add_bitcast_fusion = f32[4,8,12,96,48]{3,4,0,2,1:T(8,128)} fusion(f32[8,48,12,4,96]{4,1,3,2,0:T(8,128)S(1)} %fusion.19, f32[12,384,4,96]{1,3,2,0:T(8,128)S(1)} %fusion.13, f32[12,384,4,96]{1,3,2,0:T(8,128)} %fusion.11, s32[8,48]{1,0:T(8,128)S(1)} %multiply_add_fusion), kind=kOutput, calls=%fused_computation.5 | convolution fusion | flops 8158740480 | bytes 28313088 | tf_op jit(solution)/shard_map/kmix,qlm->iqkxl/dot_general | solution.py:12
  1051.2 14.8 copy.43
  1065.9 19.0 %reshape.239 = f32[32,12,4608]{2,1,0:T(8,128)} reshape(f32[4,8,12,96,48]{4,3,2,1,0:T(8,128)} %copy.43) | data formatting | bytes 14155776 | tf_op jit(solution)/shard_map/reshape | solution.py:98
  1089.1 31.1 %subtract_bitcast_fusion = f32[4,8,12,96,48]{3,4,0,2,1:T(8,128)} fusion(f32[8,48,12,4,96]{4,1,3,2,0:T(8,128)} %copy-done.4, f32[12,384,4,96]{1,3,2,0:T(8,128)} %copy-done.2, f32[12,384,4,96]{1,3,2,0:T(8,128)} %copy-done.5, s32[8,48]{1,0:T(8,128)S(1)} %multiply_add_fusion), kind=kOutput, calls=%fused_computation.6 | convolution fusion | flops 8158740480 | bytes 28313088 | tf_op jit(solution)/shard_map/kmix,qlm->iqkxl/dot_general | solution.py:12
  1120.2 14.8 copy.42
  1134.9 19.0 %reshape.238 = f32[32,12,4608]{2,1,0:T(8,128)} reshape(f32[4,8,12,96,48]{4,3,2,1,0:T(8,128)} %copy.42) | data formatting | bytes 14155776 | tf_op jit(solution)/shard_map/reshape | solution.py:97
  1154.0 142.4 %all-to-all-done.3 = f32[32,12,4608]{2,1,0:T(8,128)} async-done(((f32[32,12,4608]{2,1,0:T(8,128)}), f32[32,12,4608]{2,1,0:T(8,128)}, u32[]{:S(2)}, u32[]{:S(2)}) %all-to-all-start.3) | async-done | bytes 7077920 | tf_op jit(solution)/shard_map/all_to_all | solution.py:102
  1308.3 199.0 %all-to-all-done.2 = f32[32,12,4608]{2,1,0:T(8,128)} async-done(((f32[32,12,4608]{2,1,0:T(8,128)}), f32[32,12,4608]{2,1,0:T(8,128)}, u32[]{:S(2)}, u32[]{:S(2)}) %all-to-all-start.2) | async-done | bytes 7077920 | tf_op jit(solution)/shard_map/all_to_all | solution.py:101
  1515.5 23.8 %fusion.23 = f32[4608,384]{1,0:T(8,128)S(1)} fusion(f32[384,4608]{1,0:T(8,128)} %reshape.191, f32[384,4608]{1,0:T(8,128)} %reshape.193), kind=kOutput, calls=%fused_computation.39 | convolution fusion | flops 8156823552 | bytes 21233664 | tf_op jit(solution)/shard_map/ka,kz->az/dot_general | solution.py:12
  1539.4 18.7 %fusion.4 = f32[4608,384]{1,0:T(8,128)S(1)} fusion(f32[4608,384]{1,0:T(8,128)S(1)} %fusion.23, f32[384,4608]{1,0:T(8,128)S(1)} %copy-done.1), kind=kOutput, calls=%fused_computation.15 | convolution fusion | flops 8160509952 | bytes 21233664 | tf_op jit(solution)/shard_map/ka,kz->az/dot_general | solution.py:12
  1558.1 22.3 %divide_clamp_fusion = f32[4608,384]{1,0:T(8,128)} fusion(f32[4608,384]{1,0:T(8,128)S(1)} %fusion.4, f32[4608,384]{1,0:T(8,128)S(1)} %fusion.23, f32[384,4608]{1,0:T(8,128)S(1)} %bitcast.188), kind=kOutput, calls=%fused_computation.38 | convolution fusion | flops 8162279424 | bytes 28311552 | tf_op jit(solution)/shard_map/ka,kz->az/dot_general | solution.py:12
  (56 shorter events, 94.3 us)
Async XLA Ops:
  226.4 27.8 %copy-start.6 = (f32[4608,384]{1,0:T(8,128)S(1)}, f32[4608,384]{1,0:T(8,128)}, u32[]{:S(2)}) copy-start(f32[4608,384]{1,0:T(8,128)} %reshape.184) | copy-start | bytes 21233668
  251.2 2.9 copy-start.3
  288.2 211.2 %all-to-all-start.1 = ((f32[32,12,4608]{2,1,0:T(8,128)}), f32[32,12,4608]{2,1,0:T(8,128)}, u32[]{:S(2)}, u32[]{:S(2)}) async-start(f32[32,12,4608]{2,1,0:T(8,128)} %reshape.188), calls=%async_computation.1 | async-start | bytes 18874368 | tf_op jit(solution)/shard_map/all_to_all | solution.py:82
  499.4 211.3 %all-to-all-start = ((f32[32,12,4608]{2,1,0:T(8,128)}), f32[32,12,4608]{2,1,0:T(8,128)}, u32[]{:S(2)}, u32[]{:S(2)}) async-start(f32[32,12,4608]{2,1,0:T(8,128)} %reshape.186), calls=%async_computation | async-start | bytes 18874368 | tf_op jit(solution)/shard_map/all_to_all | solution.py:81
  736.5 26.2 %copy-start = (f32[12,4,8,96,48]{4,3,2,1,0:T(8,128)S(1)}, f32[12,4,8,96,48]{4,3,2,1,0:T(8,128)}, u32[]{:S(2)}) copy-start(f32[12,4,8,96,48]{4,3,2,1,0:T(8,128)} %reshape.187) | copy-start | bytes 21233668
  813.4 25.1 %copy-start.7 = (f32[12,4,96,384,1]{3,2,4,1,0:T(8,128)S(1)}, f32[12,4,96,384,1]{3,2,4,1,0:T(8,128)}, u32[]{:S(2)}) copy-start(f32[12,4,96,384,1]{3,2,4,1,0:T(8,128)} %fusion) | copy-start | bytes 21233668
  813.4 96.7 %slice-start = ((s8[7077888]{0:T(1024)(128)(4,1)}), s8[4194304]{0:T(1024)(128)(4,1)S(1)}, s32[]{:S(2)}) async-start(s8[7077888]{0:T(1024)(128)(4,1)} %bitcast.185), calls=%async_computation.4 | async-start | bytes 8388608
  838.5 50.9 %copy-start.9 = (f32[12,384,384,1]{2,1,3,0:T(8,128)}, f32[12,384,384,1]{2,1,3,0:T(8,128)S(1)}, u32[]{:S(2)}) copy-start(f32[12,384,384,1]{2,1,3,0:T(8,128)S(1)} %fusion.27) | copy-start | bytes 21233668
  838.5 71.6 %slice-start.1 = ((s8[7077888]{0:T(1024)(128)(4,1)}), s8[2883584]{0:T(1024)(128)(4,1)S(1)}, s32[]{:S(2)}) async-start(s8[7077888]{0:T(1024)(128)(4,1)} %bitcast.185), calls=%async_computation.5 | async-start | bytes 5767168
  960.8 3.0 copy-start.8
  978.2 44.5 %copy-start.2 = (f32[12,384,4,96]{1,3,2,0:T(8,128)}, f32[12,384,4,96]{1,3,2,0:T(8,128)S(1)}, u32[]{:S(2)}) copy-start(f32[12,384,4,96]{1,3,2,0:T(8,128)S(1)} %fusion.13) | copy-start | bytes 21233668
  998.3 24.5 %copy-start.5 = (f32[12,384,4,96]{1,3,2,0:T(8,128)}, f32[12,384,4,96]{1,3,2,0:T(8,128)S(1)}, u32[]{:S(2)}) copy-start(f32[12,384,4,96]{1,3,2,0:T(8,128)S(1)} %fusion.9) | copy-start | bytes 21233668
  1022.7 3.7 copy-start.4
  1084.9 211.4 %all-to-all-start.3 = ((f32[32,12,4608]{2,1,0:T(8,128)}), f32[32,12,4608]{2,1,0:T(8,128)}, u32[]{:S(2)}, u32[]{:S(2)}) async-start(f32[32,12,4608]{2,1,0:T(8,128)} %reshape.239), calls=%async_computation.3 | async-start | bytes 18874368 | tf_op jit(solution)/shard_map/all_to_all | solution.py:102
  1296.3 211.0 %all-to-all-start.2 = ((f32[32,12,4608]{2,1,0:T(8,128)}), f32[32,12,4608]{2,1,0:T(8,128)}, u32[]{:S(2)}, u32[]{:S(2)}) async-start(f32[32,12,4608]{2,1,0:T(8,128)} %reshape.238), calls=%async_computation.2 | async-start | bytes 18874368 | tf_op jit(solution)/shard_map/all_to_all | solution.py:101
  1515.5 23.9 %copy-start.1 = (f32[384,4608]{1,0:T(8,128)S(1)}, f32[384,4608]{1,0:T(8,128)}, u32[]{:S(2)}) copy-start(f32[384,4608]{1,0:T(8,128)} %reshape.191) | copy-start | bytes 21233668
  1515.5 42.5 %slice-start.2 = ((s8[7077888]{0:T(1024)(128)(4,1)}), s8[4194304]{0:T(1024)(128)(4,1)S(1)}, s32[]{:S(2)}) async-start(s8[7077888]{0:T(1024)(128)(4,1)} %bitcast.187), calls=%async_computation.6 | async-start | bytes 8388608
  1539.4 18.7 %slice-start.3 = ((s8[7077888]{0:T(1024)(128)(4,1)}), s8[2883584]{0:T(1024)(128)(4,1)S(1)}, s32[]{:S(2)}) async-start(s8[7077888]{0:T(1024)(128)(4,1)} %bitcast.187), calls=%async_computation.7 | async-start | bytes 5767168
where the time goes:
time: 1590 us; the launch traced here: 1580 us
  waiting for transfers between devices  677 us (43%)
  matrix products  484 us (30%)
  local copies, waits for them, and re-layouts  184 us (12%)
  other arithmetic  180 us (11%)
  blocking collectives  39 us (2%)
    dot_general x18, matrix products, product(): return jnp.einsum(form, left, right, precision=lax.Precision.HIGHEST)  484 us
    all_to_all x1, waiting for transfers between devices, on_device(): lax.all_to_all(sent[0], ('px', 'py'), split_axis=0, concat_axis=1, tiled=...  199 us
    scatter-add x1, other arithmetic, paint(): return empty.at[cell_rows.reshape(-1)].add(weights.reshape(-1))  175 us
    all_to_all x1, waiting for transfers between devices, on_device(): lax.all_to_all(sent[1], ('px', 'py'), split_axis=0, concat_axis=2, tiled=...  170 us
    all_to_all x1, waiting for transfers between devices, on_device(): lax.all_to_all(sent[0], ('px', 'py'), split_axis=0, concat_axis=2, tiled=...  165 us
    all_to_all x1, waiting for transfers between devices, on_device(): lax.all_to_all(sent[1], ('px', 'py'), split_axis=0, concat_axis=1, tiled=...  142 us
    reshape x2, local copies, waits for them, and re-layouts, on_device(): back_imag.reshape(devices_all, slab_planes, rows_x * rows_y)  33.8 us
    reshape x2, local copies, waits for them, and re-layouts, on_device(): back_real.reshape(devices_all, slab_planes, rows_x * rows_y)  33.8 us
  transfers between devices with their start and end apart: 4, of which 4 were waited for; matrix products, arithmetic and copies ran while one was open for 10% of the time, Pallas kernels for 0%

commit v1 on v0

v1 whole, which is shorter than its diff:
```python
import jax
import jax.numpy as jnp
import numpy as np
from jax import lax
from jax.sharding import PartitionSpec as P

CAP = 4
RADIUS = 20


def product(form, left, right):
    return jnp.einsum(form, left, right, precision=lax.Precision.HIGH)


def hartley(length):
    index_row = np.arange(length)
    angle = (index_row[:, None] * index_row[None, :] % length) * (2.0 * np.pi / length)
    return ((np.cos(angle) + np.sin(angle)) / np.sqrt(length)).astype(np.float32)


def top_hat(freq_x, freq_y, freq_z, grid):
    radial = jnp.sqrt(freq_x * freq_x + freq_y * freq_y + freq_z * freq_z) * (
        2.0 * jnp.pi * RADIUS / grid
    )
    safe = jnp.where(radial > 0, radial, 1.0)
    value = 3.0 * (jnp.sin(safe) - safe * jnp.cos(safe)) / (safe * safe * safe)
    return jnp.where(radial > 0, value, 1.0)


def on_device(photons, halo_cells, halo_counts, owners, density):
    rows_x, rows_y, grid = density.shape
    slots = photons.shape[1]
    count_x = lax.axis_size("px")
    count_y = lax.axis_size("py")
    place_y = lax.axis_index("py")
    devices_all = count_x * count_y
    planes = grid // devices_all
    area = rows_x * rows_y
    table = jnp.asarray(hartley(grid))
    table_x = table.reshape(count_x, rows_x, grid)
    table_y = table.reshape(count_y, rows_y, grid)

    def signed(index_values):
        return jnp.where(index_values < grid // 2, index_values, index_values - grid).astype(
            jnp.float32
        )

    freq = signed(jnp.arange(grid, dtype=jnp.int32))
    freq_z = signed(
        lax.axis_index(("px", "py")) * planes + jnp.arange(planes, dtype=jnp.int32)
    )
    window = top_hat(freq_z[:, None, None], freq[None, :, None], freq[None, None, :], grid)

    def smooth(field_rows):
        spec = product("az,zk->ka", field_rows, table)
        got = lax.all_to_all(
            spec.reshape(devices_all, planes, area),
            ("px", "py"), split_axis=0, concat_axis=0, tiled=True,
        )
        got = got.reshape(count_x, count_y, planes, rows_y, rows_x)
        half = product("iqklx,ixn->qkln", got, table_x)
        full = product("qkln,qlm->kmn", half, table_y) * window
        half = product("kmn,qlm->qkln", full, table_y)
        back = product("qkln,ixn->iqklx", half, table_x)
        got = lax.all_to_all(
            back.reshape(devices_all, planes, area),
            ("px", "py"), split_axis=0, concat_axis=0, tiled=True,
        )
        return product("ka,kz->az", got.reshape(grid, area), table)

    density_rows = density.transpose(1, 0, 2).reshape(area, grid)
    density_smooth = smooth(density_rows)

    slot_index = jnp.arange(slots, dtype=jnp.int32)[None, :]
    weights = jnp.where(slot_index < halo_counts[:, None], photons, 0.0)
    all_weights = lax.all_gather(weights, "py", axis=0, tiled=True)
    all_cells = lax.all_gather(halo_cells, "py", axis=0, tiled=True)
    all_owners = lax.all_gather(owners, "py", axis=0, tiled=True)[:, 0]
    owned = all_owners == place_y
    chosen = jnp.argsort(jnp.where(owned, 0, 1), stable=True)[: CAP * count_y]
    own_weights = jnp.where(owned[chosen][:, None], all_weights[chosen], 0.0)
    own_cells = all_cells[chosen]
    row = own_cells // grid
    spot = ((row % rows_y) * rows_x + row // rows_y) * grid + own_cells % grid
    painted = jnp.zeros((area * grid,), jnp.float32)
    painted = painted.at[spot.reshape(-1)].add(own_weights.reshape(-1))
    photon_smooth = smooth(painted.reshape(area, grid))

    fraction = jnp.clip(photon_smooth / jnp.maximum(density_smooth, 0.5), 0.0, 1.0)
    return fraction.reshape(rows_y, rows_x, grid).transpose(1, 0, 2)


def solution(mesh):
    placed = (
        P(("px", "py"), None),
        P(("px", "py"), None),
        P(("px", "py")),
        P(("px", "py"), None),
        P("px", "py", None),
    )
    return jax.shard_map(
        on_device, mesh=mesh, in_specs=placed, out_specs=P("px", "py", None), check_vma=False
    )
```

time: 1590 us -> 992 us (0.62)
  matrix products: 484 us -> 165 us
  waiting for transfers between devices: 677 us -> 423 us
  blocking collectives: 39 us -> 233 us
  other arithmetic: 180 us -> 28.9 us
  local copies, waits for them, and re-layouts: 184 us -> 112 us
    dot_general x18 -> x12, matrix products: 484 us -> 165 us  [product(): return jnp.einsum(form, left, right, precision=lax.Precision.HIGH)]
    all_to_all x4, waiting for transfers between devices: 677 us -> 423 us  [the longest x2 306 us: smooth(): lax.all_to_all(back.reshape(devices_all, planes, area), ('px', 'py'), spl...]
    unnamed x1, blocking collectives: 8.89 us -> 205 us
    scatter-add x1, other arithmetic: 175 us -> 25.3 us  [on_device(): painted = painted.at[spot.reshape(-1)].add(own_weights.reshape(-1))]
    reshape x11, local copies, waits for them, and re-layouts: 150 us -> 95.8 us  [the longest x4 33.2 us: smooth(): back.reshape(devices_all, planes, area)]
    all_to_all x2 -> x0, local copies, waits for them, and re-layouts: 21.5 us -> none  [the longest x1 10.7 us: on_device(): lax.all_to_all(sent[1], ('px', 'py'), split_axis=0, concat_axis=2, tiled=...]
  transfers between devices with their start and end apart: 4 -> 4, of which waited for: 4 -> 3; matrix products, arithmetic and copies ran while one was open for 10% -> 26% of each run, Pallas kernels for 0% -> 0%
where the time goes in v1:
time: 992 us; the launch traced here: 982 us
  waiting for transfers between devices  423 us (43%)
  blocking collectives  233 us (23%)
  matrix products  165 us (17%)
  local copies, waits for them, and re-layouts  112 us (11%)
  other arithmetic  28.9 us (3%)
  starting transfers between devices  19.3 us (2%)
    all_to_all x2, waiting for transfers between devices, smooth(): lax.all_to_all(back.reshape(devices_all, planes, area), ('px', 'py'), spl...  306 us
    unnamed x1, blocking collectives  205 us
    dot_general x12, matrix products, product(): return jnp.einsum(form, left, right, precision=lax.Precision.HIGH)  165 us
    all_to_all x2, waiting for transfers between devices, smooth(): lax.all_to_all(spec.reshape(devices_all, planes, area), ('px', 'py'), spl...  117 us
    reshape x4, local copies, waits for them, and re-layouts, smooth(): back.reshape(devices_all, planes, area)  33.2 us
    scatter-add x1, other arithmetic, on_device(): painted = painted.at[spot.reshape(-1)].add(own_weights.reshape(-1))  25.3 us
    reshape x2, local copies, waits for them, and re-layouts, smooth(): got = got.reshape(count_x, count_y, planes, rows_y, rows_x)  22.3 us
  transfers between devices with their start and end apart: 4, of which 3 were waited for; matrix products, arithmetic and copies ran while one was open for 26% of the time, Pallas kernels for 0%

profile of v1, /device:TPU:0, one launch (start us, length us, event | category | flops | bytes accessed | tf_op | source)
XLA Modules:
  0.0 981.9 jit_solution(13321077338012238784)
XLA Ops:
  0.0 5.3 copy.31
  5.4 6.2 fusion.49
  11.5 8.0 copy.32
  19.5 7.4 all-to-all-start.2
  28.4 204.8 %all-reduce = s32[256]{0:T(256)S(1)} all-reduce(s32[256]{0:T(256)S(1)} %bitcast_dynamic-update-slice_fusion), channel_id=1, replica_groups=mesh['px'=4,'py'=8] {'py'}, use_global_device_ids=true, to_apply=%add | all-reduce | flops 256 | bytes 2048
  237.1 13.9 %all_gather.11 = f32[256,128]{1,0:T(8,128)S(1)} all-gather(f32[32,128]{1,0:T(8,128)S(1)} %fusion.35), channel_id=1, replica_groups=mesh['px'=4,'py'=8] {'py'}, dimensions={0}, use_global_device_ids=true | all-gather | bytes 147456 | tf_op jit(solution)/shard_map/all_gather | solution.py:76
  251.7 14.0 %all_gather.9 = s32[256,128]{1,0:T(8,128)S(1)} all-gather(s32[32,128]{1,0:T(8,128)S(1)} %copy-done.3), channel_id=1, replica_groups=mesh['px'=4,'py'=8] {'py'}, dimensions={0}, use_global_device_ids=true | all-gather | bytes 147456 | tf_op jit(solution)/shard_map/all_gather | solution.py:77
  266.5 25.3 %scatter_custom_fusion = f32[1769472]{0:T(1024)} fusion(s32[4096]{0:T(1024)S(1)} %bitcast.122, f32[4096]{0:T(1024)S(1)} %select_bitcast_fusion, f32[]{:T(128)} %constant.26.clone.1), kind=kCustom, calls=%fused_computation.29 | custom fusion | flops 4096 | bytes 7077892 | tf_op jit(solution)/shard_map/scatter-add | solution.py:86
  291.8 8.9 reshape.232
  300.7 12.5 %fusion.48 = f32[384,4608]{1,0:T(8,128)} fusion(f32[384,384]{1,0:T(8,128)S(1)} %copy-done.1, f32[4608,384]{1,0:T(8,128)} %reshape.232), kind=kOutput, calls=%fused_computation.73 | convolution fusion | flops 4076863488 | bytes 14745600 | tf_op jit(solution)/shard_map/az,zk->ka/dot_general | solution.py:12
  313.2 8.0 reshape.233
  325.4 11.2 %reshape.300 = f32[4,8,12,48,96]{4,3,2,1,0:T(8,128)} reshape(f32[32,12,4608]{2,1,0:T(8,128)} %all-to-all-done.2) | data formatting | bytes 14155776 | tf_op jit(solution)/shard_map/reshape | solution.py:60
  336.6 11.5 %fusion.26 = f32[8,12,48,384,1]{3,2,1,0,4:T(8,128)S(1)} fusion(f32[4,8,12,48,96]{4,3,2,1,0:T(8,128)} %reshape.300, f32[4,96,384,1,1]{2,1,0,4,3:T(8,128)S(1)} %copy-done), kind=kOutput, calls=%fused_computation.33 | convolution fusion | flops 4076863488 | bytes 14745600 | tf_op jit(solution)/shard_map/iqklx,ixn->qkln/dot_general | solution.py:12
  348.1 7.7 fusion.4
  355.8 34.7 %fusion.11 = f32[12,384,8,48]{1,3,0,2:T(8,128)S(1)} fusion(f32[8,48,384,1]{2,1,3,0:T(8,128)S(1)} %copy-done.7, f32[12,384,384,1]{2,1,0,3:T(8,128)S(1)} %fusion.4, f32[384]{0:T(512)S(1)} %fusion.37, f32[12,384]{1,0:T(8,128)S(1)} %broadcast_add_fusion), kind=kOutput, calls=%fused_computation.21 | convolution fusion | flops 4098097152 | bytes 14765568 | tf_op jit(solution)/shard_map/kmn,qlm->qkln/dot_general | solution.py:12
  390.5 8.0 fusion.23
  398.6 4.9 copy.54
  403.5 11.7 %reshape.301 = f32[32,12,4608]{2,1,0:T(8,128)} reshape(f32[4,8,12,48,96]{4,3,2,1,0:T(8,128)} %copy.54) | data formatting | bytes 14155776 | tf_op jit(solution)/shard_map/reshape | solution.py:66
  415.1 117.4 %all-to-all-done = f32[32,12,4608]{2,1,0:T(8,128)} async-done(((f32[32,12,4608]{2,1,0:T(8,128)}), f32[32,12,4608]{2,1,0:T(8,128)}, u32[]{:S(2)}, u32[]{:S(2)}) %all-to-all-start) | async-done | bytes 7077920 | tf_op jit(solution)/shard_map/all_to_all | solution.py:56
  536.4 11.1 %reshape.298 = f32[4,8,12,48,96]{4,3,2,1,0:T(8,128)} reshape(f32[32,12,4608]{2,1,0:T(8,128)} %all-to-all-done) | data formatting | bytes 14155776 | tf_op jit(solution)/shard_map/reshape | solution.py:60
  547.6 11.4 %fusion.28 = f32[8,12,48,384,1]{3,2,1,0,4:T(8,128)S(1)} fusion(f32[4,8,12,48,96]{4,3,2,1,0:T(8,128)} %reshape.298, f32[4,96,384,1,1]{2,1,0,4,3:T(8,128)S(1)} %copy-done), kind=kOutput, calls=%fused_computation.35 | convolution fusion | flops 4076863488 | bytes 14745600 | tf_op jit(solution)/shard_map/iqklx,ixn->qkln/dot_general | solution.py:12
  559.0 7.7 fusion.6
  566.6 34.7 %fusion.16 = f32[12,384,8,48]{1,3,0,2:T(8,128)S(1)} fusion(f32[8,48,384,1]{2,1,3,0:T(8,128)S(1)} %copy-done.7, f32[12,384,384,1]{2,1,0,3:T(8,128)S(1)} %fusion.6, f32[384]{0:T(512)S(1)} %fusion.37, f32[12,384]{1,0:T(8,128)S(1)} %broadcast_add_fusion), kind=kOutput, calls=%fused_computation.26 | convolution fusion | flops 4098097152 | bytes 14765568 | tf_op jit(solution)/shard_map/kmn,qlm->qkln/dot_general | solution.py:12
  601.4 8.0 fusion.20
  614.4 11.7 %reshape.299 = f32[32,12,4608]{2,1,0:T(8,128)} reshape(f32[4,8,12,48,96]{4,3,2,1,0:T(8,128)} %copy.50) | data formatting | bytes 14155776 | tf_op jit(solution)/shard_map/reshape | solution.py:66
  626.0 117.6 %all-to-all-done.3 = f32[32,12,4608]{2,1,0:T(8,128)} async-done(((f32[32,12,4608]{2,1,0:T(8,128)}), f32[32,12,4608]{2,1,0:T(8,128)}, u32[]{:S(2)}, u32[]{:S(2)}) %all-to-all-start.3) | async-done | bytes 7077920 | tf_op jit(solution)/shard_map/all_to_all | solution.py:65
  747.6 8.2 reshape.242
  755.8 11.0 %convolution_maximum_fusion = f32[4608,384]{1,0:T(8,128)} fusion(f32[384,4608]{1,0:T(8,128)} %reshape.242, f32[384,384]{1,0:T(8,128)S(1)} %copy-done.1), kind=kOutput, calls=%fused_computation.8 | convolution fusion | flops 4078632960 | bytes 14745600 | tf_op jit(solution)/shard_map/ka,kz->az/dot_general | solution.py:12
  766.8 188.0 %all-to-all-done.1 = f32[32,12,4608]{2,1,0:T(8,128)} async-done(((f32[32,12,4608]{2,1,0:T(8,128)}), f32[32,12,4608]{2,1,0:T(8,128)}, u32[]{:S(2)}, u32[]{:S(2)}) %all-to-all-start.1) | async-done | bytes 7077920 | tf_op jit(solution)/shard_map/all_to_all | solution.py:65
  954.8 8.2 reshape.238
  963.0 11.5 %divide_clamp_fusion = f32[4608,384]{1,0:T(8,128)S(1)} fusion(f32[4608,384]{1,0:T(8,128)} %convolution_maximum_fusion, f32[384,4608]{1,0:T(8,128)} %reshape.238, f32[384,384]{1,0:T(8,128)S(1)} %copy-done.1), kind=kOutput, calls=%fused_computation.28 | convolution fusion | flops 4080402432 | bytes 21823488 | tf_op jit(solution)/shard_map/ka,kz->az/dot_general | solution.py:12
  974.5 7.1 copy.62
  (42 shorter events, 23.0 us)
Async XLA Ops:
  0.0 5.4 copy-start.2
  19.5 7.5 copy-start.8
  19.5 8.7 copy-start.6
  19.5 217.5 %copy-start.4 = (f32[32,128]{1,0:T(8,128)S(1)}, f32[32,128]{1,0:T(8,128)}, u32[]{:S(2)}) copy-start(f32[32,128]{1,0:T(8,128)} %param.6) | copy-start | bytes 49156
  19.5 217.5 %copy-start.5 = (s32[32]{0:T(128)S(1)}, s32[32]{0:T(128)}, u32[]{:S(2)}) copy-start(s32[32]{0:T(128)} %param.8) | copy-start | bytes 388
  19.5 232.1 %copy-start.3 = (s32[32,128]{1,0:T(8,128)S(1)}, s32[32,128]{1,0:T(8,128)}, u32[]{:S(2)}) copy-start(s32[32,128]{1,0:T(8,128)} %param.7) | copy-start | bytes 49156
  19.5 301.7 %all-to-all-start.2 = ((f32[32,12,4608]{2,1,0:T(8,128)}), f32[32,12,4608]{2,1,0:T(8,128)}, u32[]{:S(2)}, u32[]{:S(2)}) async-start(f32[32,12,4608]{2,1,0:T(8,128)} %copy.32), calls=%async_computation.2 | async-start | bytes 18874368 | tf_op jit(solution)/shard_map/all_to_all | solution.py:56
  291.8 8.9 copy-start.1
  321.2 211.4 %all-to-all-start = ((f32[32,12,4608]{2,1,0:T(8,128)}), f32[32,12,4608]{2,1,0:T(8,128)}, u32[]{:S(2)}, u32[]{:S(2)}) async-start(f32[32,12,4608]{2,1,0:T(8,128)} %reshape.233), calls=%async_computation | async-start | bytes 18874368 | tf_op jit(solution)/shard_map/all_to_all | solution.py:56
  325.4 11.2 %copy-start = (f32[4,96,384,1,1]{2,1,0,4,3:T(8,128)S(1)}, f32[4,96,384,1,1]{2,1,0,4,3:T(8,128)}, u32[]{:S(2)}) copy-start(f32[4,96,384,1,1]{2,1,0,4,3:T(8,128)} %constant.88) | copy-start | bytes 1769476
  336.6 11.5 %copy-start.7 = (f32[8,48,384,1]{2,1,3,0:T(8,128)S(1)}, f32[8,48,384,1]{2,1,3,0:T(8,128)}, u32[]{:S(2)}) copy-start(f32[8,48,384,1]{2,1,3,0:T(8,128)} %constant.89) | copy-start | bytes 1769476
  532.6 211.1 %all-to-all-start.3 = ((f32[32,12,4608]{2,1,0:T(8,128)}), f32[32,12,4608]{2,1,0:T(8,128)}, u32[]{:S(2)}, u32[]{:S(2)}) async-start(f32[32,12,4608]{2,1,0:T(8,128)} %reshape.301), calls=%async_computation.3 | async-start | bytes 18874368 | tf_op jit(solution)/shard_map/all_to_all | solution.py:65
  743.7 211.2 %all-to-all-start.1 = ((f32[32,12,4608]{2,1,0:T(8,128)}), f32[32,12,4608]{2,1,0:T(8,128)}, u32[]{:S(2)}, u32[]{:S(2)}) async-start(f32[32,12,4608]{2,1,0:T(8,128)} %reshape.299), calls=%async_computation.1 | async-start | bytes 18874368 | tf_op jit(solution)/shard_map/all_to_all | solution.py:65
